TPU v7x, 512 devices: a whole 4x4x16 slice. The times are simulated.
512 devices in a mesh: tm: 16 (over y, x_hi, core), feed: 32 (over x_lo, z).
Axes of the slice: x: 4 (x_hi: 2, x_lo: 2; x = x_hi * 2 + x_lo), y: 4, z: 16, core: 2. Of those that a mesh axis runs over, the one named last changes fastest.
Arguments:
- voltages: bfloat16 [48, 1024, 16384], P('tm', 'feed'), may hold values from -6 to 6
- pfb_taps: float32 [4, 16384], replicated, may hold values from 0.2 to 1
- feed_of_slot: int32 [1024], replicated, may hold values from 0 to 1023, each once
Outputs:
- beam_power: float32 [16, 1024, 8192], P('tm', None, 'feed')
Inputs may be any that keep to these rules, and one draw needn't show every extreme that they name: feed_of_slot[256 * r + j] is the feed at position j of cylinder r; every feed stands at exactly one position.
All inputs are finite; a program needn't handle non-finite values.
Results may differ from a plain program's by a relative error of at most 0.0052.
Values may be sent and summed in bfloat16 or wider, within the bound.
A program may use at most 64 MiB of HBM per device.

v0:
```python
import math

import jax
import jax.numpy as jnp
from jax import lax
from jax.sharding import PartitionSpec as P

CYLINDERS = 4
COL_FEEDS = 256
SECTION_ONE = 128
SECTION_TWO = 128


def passed_along(array, axis, by):
    peers = lax.axis_size(axis)
    pairs = [(i, i + by) for i in range(peers) if 0 <= i + by < peers]
    return lax.ppermute(array, axis, pairs)


def tables(columns, row_count, period, factor):
    row_index = jnp.arange(row_count, dtype=jnp.int32)[:, None]
    col_index = jnp.arange(columns, dtype=jnp.int32)[None, :]
    angles = (row_index * col_index % period).astype(jnp.float32) * (2.0 * math.pi / period)
    return (jnp.cos(angles) * factor, -jnp.sin(angles) * factor)


def complex_table(part_re, part_im):
    upper = jnp.stack([part_re, -part_im], axis=1)
    lower = jnp.stack([part_im, part_re], axis=1)
    return jnp.stack([upper, lower], axis=1)


def tap_sum(weights, blocks, count):
    total = weights[0] * blocks[0:count].astype(jnp.float32)
    for tap_index in range(1, weights.shape[0]):
        total = total + weights[tap_index] * blocks[tap_index : tap_index + count].astype(
            jnp.float32
        )
    return total


def on_device(voltages, pfb_taps, feed_of_slot):
    spectra_here = voltages.shape[0]
    feeds_here = voltages.shape[1]
    weights = pfb_taps[:, None, None, :]
    arrived = passed_along(voltages, "tm", -1)
    extended = jnp.concatenate([voltages, arrived], axis=0)
    framed = tap_sum(weights, extended, spectra_here).astype(jnp.bfloat16)
    framed = framed.reshape(spectra_here, feeds_here, SECTION_ONE, SECTION_TWO)
    f32 = jnp.float32
    one_re, one_im = tables(SECTION_ONE, SECTION_ONE, SECTION_ONE, 1.0)
    one_both = jnp.concatenate([one_re, one_im], axis=0).astype(jnp.bfloat16)
    first = jnp.einsum("kn,sfnm->sfkm", one_both, framed, preferred_element_type=f32)
    first_re = first[:, :, :SECTION_ONE, :]
    first_im = first[:, :, SECTION_ONE:, :]
    twist_re, twist_im = tables(SECTION_TWO, SECTION_ONE, SECTION_ONE * SECTION_TWO, 1.0)
    factor = 1.0 / math.sqrt(SECTION_ONE * SECTION_TWO)
    turned = jnp.concatenate(
        [
            ((first_re * twist_re - first_im * twist_im) * factor).astype(jnp.bfloat16),
            ((first_re * twist_im + first_im * twist_re) * factor).astype(jnp.bfloat16),
        ],
        axis=-1,
    )
    two_re, two_im = tables(SECTION_TWO, SECTION_TWO // 2, SECTION_TWO, 1.0)
    two_table = (
        complex_table(two_re, two_im)
        .reshape(SECTION_TWO // 2, 2, 2 * SECTION_TWO)
        .astype(jnp.bfloat16)
    )
    spectrum = jnp.einsum("qem,sfkm->sfqek", two_table, turned, preferred_element_type=f32).astype(
        jnp.bfloat16
    )
    spectrum = spectrum.reshape(spectra_here, feeds_here, SECTION_TWO // 2, 2 * SECTION_ONE)
    col_re, col_im = tables(COL_FEEDS, COL_FEEDS, COL_FEEDS, 1.0 / math.sqrt(COL_FEEDS))
    col_table = complex_table(col_re, col_im).astype(jnp.bfloat16)
    cyl_re, cyl_im = tables(CYLINDERS, CYLINDERS, CYLINDERS, 1.0 / math.sqrt(CYLINDERS))
    cyl_table = complex_table(cyl_re, cyl_im)
    highest = lax.Precision.HIGHEST
    received = lax.all_to_all(spectrum, "feed", split_axis=2, concat_axis=1, tiled=True)
    spectra = received.shape[0]
    owned = received.shape[2]
    shape = (spectra, CYLINDERS, COL_FEEDS, owned, 2, SECTION_ONE)
    grid = jnp.take(received, feed_of_slot, axis=1).reshape(shape)
    along = jnp.einsum("pedj,scjqdk->scpqek", col_table, grid, preferred_element_type=f32)
    beam = jnp.einsum("medc,scpqdk->smpqek", cyl_table, along, precision=highest)
    energy = (
        beam[:, :, :, :, 0, :] * beam[:, :, :, :, 0, :]
        + beam[:, :, :, :, 1, :] * beam[:, :, :, :, 1, :]
    )
    powers = energy.reshape(spectra, CYLINDERS * COL_FEEDS, owned * SECTION_ONE)
    return jnp.sum(powers, axis=0, keepdims=True)


def solution(mesh):
    in_specs = (P("tm", "feed", None), P(), P())
    out_specs = P("tm", None, "feed")
    return jax.shard_map(
        on_device, mesh=mesh, in_specs=in_specs, out_specs=out_specs, check_vma=False
    )
```

profile of v0, /device:TPU:49, one launch (start us, length us, event | category | flops | bytes accessed | tf_op | source)
XLA Modules:
  0.0 286.2 jit_solution(13419982797585444049)
XLA Ops:
  0.0 2.8 collective-permute-start
  2.8 3.7 %constant_dynamic-update-slice_fusion.1 = bf16[6,32,16384]{2,1,0:T(8,128)(2,1)} fusion(bf16[3,32,16384]{2,1,0:T(8,128)(2,1)} %param.3), kind=kLoop, calls=%fused_computation.87 | loop fusion | bytes 6291456
  11.2 1.4 pad_maximum_fusion
  13.3 1.4 stack.65
  14.7 1.4 copy.64
  16.1 1.4 stack.67
  17.6 23.1 %collective-permute-done = bf16[3,32,16384]{2,1,0:T(8,128)(2,1)} collective-permute-done((bf16[3,32,16384]{2,1,0:T(8,128)(2,1)}, bf16[3,32,16384]{2,1,0:T(8,128)(2,1)}, u32[]{:S(2)}, u32[]{:S(2)}) %collective-permute-start) | collective-permute-done | bytes 3145760 | tf_op jit(solution)/shard_map/ppermute | solution.py:17
  40.7 3.8 %constant_dynamic-update-slice_fusion = bf16[6,32,16384]{2,1,0:T(8,128)(2,1)} fusion(bf16[6,32,16384]{2,1,0:T(8,128)(2,1)} %constant_dynamic-update-slice_fusion.1, bf16[3,32,16384]{2,1,0:T(8,128)(2,1)} %collective-permute-done), kind=kLoop, calls=%fused_computation.86 | loop fusion | bytes 6291456 | tf_op jit(solution)/shard_map/concatenate | solution.py:47
  44.5 5.0 %add_convert_fusion = bf16[3,32,16384]{2,1,0:T(8,128)(2,1)S(1)} fusion(bf16[3,32,16384]{2,1,0:T(8,128)(2,1)} %collective-permute-done, bf16[3,32,16384]{2,1,0:T(8,128)(2,1)S(1)} %copy-done, bf16[6,32,16384]{2,1,0:T(8,128)(2,1)} %constant_dynamic-update-slice_fusion, f32[16384]{0:T(1024)S(1)} %bitcast.87, f32[16384]{0:T(1024)S(1)} %bitcast.88, ...), kind=kLoop, calls=%fused_computation.7 | loop fusion | flops 18874368 | bytes 15990784 | tf_op jit(solution)/shard_map/convert_element_type | solution.py:48
  50.4 2.4 convolution_bitcast_fusion
  52.8 2.2 multiply_convert_fusion.1
  56.2 3.2 %copy.90 = bf16[3,32,64,2,128]{4,3,1,0,2:T(2,128)(2,1)S(1)} copy(bf16[3,32,64,2,128]{4,2,3,1,0:T(8,128)(2,1)S(1)} %convert_bitcast_fusion) | data formatting | bytes 6291456 | tf_op jit(solution)/shard_map/reshape | solution.py:74
  59.5 3.8 %reshape.341 = bf16[3,32,64,256]{3,1,0,2:T(8,128)(2,1)} reshape(bf16[3,32,64,2,128]{4,3,1,0,2:T(2,128)(2,1)S(1)} %copy.90) | data formatting | bytes 6291456 | tf_op jit(solution)/shard_map/reshape | solution.py:74
  63.3 15.7 %all-to-all-start = ((bf16[3,32,64,256]{3,1,0,2:T(8,128)(2,1)}), bf16[3,32,64,256]{3,1,0,2:T(8,128)(2,1)S(1)}, u32[]{:S(2)}, u32[]{:S(2)}) async-start(bf16[3,32,64,256]{3,1,0,2:T(8,128)(2,1)} %reshape.341), calls=%async_computation | async-start | bytes 6291456 | tf_op jit(solution)/shard_map/all_to_all | solution.py:80
  82.0 141.5 %all-to-all-done = bf16[3,32,64,256]{3,1,0,2:T(8,128)(2,1)S(1)} async-done(((bf16[3,32,64,256]{3,1,0,2:T(8,128)(2,1)}), bf16[3,32,64,256]{3,1,0,2:T(8,128)(2,1)S(1)}, u32[]{:S(2)}, u32[]{:S(2)}) %all-to-all-start) | async-done | bytes 3145760 | tf_op jit(solution)/shard_map/all_to_all | solution.py:80
  223.8 3.2 %copy.70 = bf16[3,1024,2,256]{3,2,1,0:T(2,128)(2,1)S(1)} copy(bf16[3,1024,2,256]{3,1,2,0:T(8,128)(2,1)S(1)} %bitcast.82) | data formatting | bytes 6291456 | tf_op jit(solution)/shard_map/all_to_all | solution.py:80
  227.1 14.1 %gather_fusion = bf16[1024,3,2,256]{3,2,1,0:T(2,128)(2,1)} fusion(bf16[3,1024,2,256]{3,2,1,0:T(2,128)(2,1)S(1)} %copy.70, s32[1024]{0:T(1024)S(1)} %fusion.49), kind=kCustom, calls=%fused_computation | custom fusion | bytes 6295552 | tf_op jit(solution)/shard_map/jit(_take)/gather | solution.py:84
  241.2 8.5 %gather.7 = bf16[3,4,256,2,2,128]{5,4,3,0,2,1:T(2,128)(2,1)S(1)} reshape(bf16[3,1024,2,256]{3,2,0,1:T(2,128)(2,1)} %bitcast.83) | data formatting | bytes 6291456 | tf_op jit(solution)/shard_map/jit(_take)/gather | solution.py:84
  249.6 6.1 %copy.71 = bf16[3,4,256,2,2,128]{2,5,4,3,1,0:T(8,128)(2,1)} copy(bf16[3,4,256,2,2,128]{5,4,3,0,2,1:T(2,128)(2,1)S(1)} %gather.7) | data formatting | bytes 6291456 | tf_op jit(solution)/shard_map/jit(_take)/gather | solution.py:84
  255.7 6.4 %fusion.10 = f32[3,4,256,2,2,128,1]{2,5,4,3,1,0,6:T(8,128)} fusion(bf16[3,4,256,2,2,128]{2,5,4,3,1,0:T(8,128)(2,1)} %copy.71, pred[4,256]{1,0:T(4,128)(4,1)S(1)} %broadcast_in_dim.13, bf16[256,1,2,256]{3,0,2,1:T(8,128)(2,1)} %get-tuple-element.12, bf16[256,1,2,256]{3,0,2,1:T(8,128)(2,1)S(1)} %get-tuple-element.11), kind=kOutput, calls=%fused_computation.19 | convolution fusion | flops 1613234176 | bytes 9962496 | tf_op jit(solution)/shard_map/pedj,scjqdk->scpqek/dot_general | solution.py:85
  262.1 7.9 %copy.85 = f32[3,4,256,2,2,128,1]{5,1,4,6,3,2,0:T(4,128)} copy(f32[3,4,256,2,2,128,1]{2,5,4,3,1,0,6:T(8,128)} %fusion.10) | data formatting | bytes 12582912 | tf_op jit(solution)/shard_map/pedj,scjqdk->scpqek/transpose | solution.py:85
  270.0 12.7 %convolution_bitcast_fusion.1 = f32[3,4,256,2,2,128]{5,1,4,3,2,0:T(4,128)S(1)} fusion(f32[3,4,256,2,2,128,1]{5,1,4,6,3,2,0:T(4,128)} %copy.85, f32[4,1,2,4]{3,0,2,1:T(4,128)S(1)} %get-tuple-element.16, f32[4,1,2,4]{3,0,2,1:T(4,128)S(1)} %get-tuple-element.15), kind=kOutput, calls=%fused_computation.20 | convolution fusion | flops 150995008 | bytes 12583168 | tf_op jit(solution)/shard_map/medc,scpqdk->smpqek/dot_general | solution.py:86
  282.6 1.2 fusion.5
  284.4 1.8 broadcast_in_dim.17
  (36 shorter events, 11.4 us)
Async XLA Ops:
  0.0 44.5 %copy-start = (bf16[3,32,16384]{2,1,0:T(8,128)(2,1)S(1)}, bf16[3,32,16384]{2,1,0:T(8,128)(2,1)}, u32[]{:S(2)}) copy-start(bf16[3,32,16384]{2,1,0:T(8,128)(2,1)} %param.3) | copy-start | bytes 9437188
  0.0 17.5 %copy-start.1 = (f32[4,16384]{1,0:T(4,128)S(1)}, f32[4,16384]{1,0:T(4,128)}, u32[]{:S(2)}) copy-start(f32[4,16384]{1,0:T(4,128)} %param.4) | copy-start | bytes 786436
  0.0 40.7 %collective-permute-start = (bf16[3,32,16384]{2,1,0:T(8,128)(2,1)}, bf16[3,32,16384]{2,1,0:T(8,128)(2,1)}, u32[]{:S(2)}, u32[]{:S(2)}) collective-permute-start(bf16[3,32,16384]{2,1,0:T(8,128)(2,1)} %param.3), channel_id=1, source_target_pairs={{32,0},{64,32},{96,64},{128,96},{160,128},{192,160},{224,192},{256... | collective-permute-start | bytes 9437192 | tf_op jit(solution)/shard_map/ppermute | solution.py:17
  49.5 0.9 copy-start.2
  49.5 0.9 copy-start.3
  52.8 2.2 copy-start.4
  52.8 2.2 copy-start.5
  59.5 19.5 %copy-start.6 = (s32[1024]{0:T(1024)S(1)}, s32[1024]{0:T(1024)}, u32[]{:S(2)}) copy-start(s32[1024]{0:T(1024)} %param.5) | copy-start | bytes 12292
  63.3 160.2 %all-to-all-start = ((bf16[3,32,64,256]{3,1,0,2:T(8,128)(2,1)}), bf16[3,32,64,256]{3,1,0,2:T(8,128)(2,1)S(1)}, u32[]{:S(2)}, u32[]{:S(2)}) async-start(bf16[3,32,64,256]{3,1,0,2:T(8,128)(2,1)} %reshape.341), calls=%async_computation | async-start | bytes 6291456 | tf_op jit(solution)/shard_map/all_to_all | solution.py:80
where the time goes:
time: 287 us; the launch traced here: 286 us
  waiting for transfers between devices  165 us (57%)
  local copies, waits for them, and re-layouts  63.9 us (22%)
  matrix products  22.6 us (8%)
  starting transfers between devices  18.5 us (6%)
  other arithmetic  16.3 us (6%)
    all_to_all x1, waiting for transfers between devices, on_device(): lax.all_to_all(spectrum, 'feed', split_axis=2, concat_axis=1, tiled=True)  142 us
    gather x3, local copies, waits for them, and re-layouts, on_device(): grid = jnp.take(received, feed_of_slot, axis=1).reshape(shape)  28.6 us
    ppermute x1, waiting for transfers between devices, passed_along(): return lax.ppermute(array, axis, pairs)  23.1 us
    all_to_all x1, starting transfers between devices, on_device(): lax.all_to_all(spectrum, 'feed', split_axis=2, concat_axis=1, tiled=True)  15.7 us
    dot_general x1, matrix products, on_device(): jnp.einsum('medc,scpqdk->smpqek', cyl_table, along, precision=highest)  12.7 us
    transpose x1, local copies, waits for them, and re-layouts, on_device(): jnp.einsum('pedj,scjqdk->scpqek', col_table, grid, preferred_element_type...  7.87 us
    reshape x2, local copies, waits for them, and re-layouts, on_device(): spectrum.reshape(spectra_here, feeds_here, SECTION_TWO // 2, 2 * SECTION_...  7.03 us
    dot_general x1, matrix products, on_device(): jnp.einsum('pedj,scjqdk->scpqek', col_table, grid, preferred_element_type...  6.4 us
  transfers between devices with their start and end apart: 2, of which 2 were waited for; matrix products, arithmetic and copies ran while one was open for 6% of the time, Pallas kernels for 0%

commit v1 on v0

v1 whole, which is shorter than its diff:
```python
import functools
import math

import jax
import jax.numpy as jnp
import numpy as np
from jax import lax
from jax.experimental import pallas as pl
from jax.experimental.pallas import tpu as pltpu
from jax.sharding import PartitionSpec as P

CYLINDERS = 4
COL_FEEDS = 256
ONE = 128
TWO = 128
SPECTRA = 3
FEEDS = 32
PEERS = 32
RING = 16
BLOCK = ONE * TWO
BEAMS = CYLINDERS * COL_FEEDS
CHUNK = 16
CHUNKS = FEEDS // CHUNK
ROWS = 2 * CHUNK
DEPTH = 2 * PEERS * FEEDS
F32 = jnp.float32
BF16 = jnp.bfloat16


def tables(columns, row_count, period, factor):
    index = np.arange(row_count)[:, None] * np.arange(columns)[None, :] % period
    angles = index.astype(np.float32) * np.float32(2.0 * math.pi / period)
    cos = np.cos(angles.astype(np.float64)) * factor
    sin = -np.sin(angles.astype(np.float64)) * factor
    return cos.astype(np.float32), sin.astype(np.float32)


def constants():
    one = np.concatenate(tables(ONE, ONE, ONE, 1.0), axis=0)
    twist = np.stack(tables(TWO, ONE, BLOCK, 1.0 / math.sqrt(BLOCK)))
    two_re, two_im = tables(TWO, TWO // 2, TWO, 1.0)
    upper = np.stack([two_re, -two_im], axis=1)
    lower = np.stack([two_im, two_re], axis=1)
    two = np.stack([upper, lower], axis=1).reshape(TWO, 2 * TWO)
    col = np.concatenate(tables(COL_FEEDS, COL_FEEDS, COL_FEEDS, 1.0 / math.sqrt(COL_FEEDS)), axis=0)
    half = 1.0 / math.sqrt(CYLINDERS)
    return (
        jnp.asarray(one).astype(BF16),
        jnp.asarray(twist),
        jnp.asarray(two).astype(BF16),
        jnp.asarray(col).astype(BF16) * jnp.asarray(half, BF16),
    )


def peer_at(me, dx, dz):
    x_lo, z = me // RING, me % RING
    return ((x_lo + dx) % 2) * RING + (z + dz) % RING


def kernel(
    volts,
    taps_in,
    feeds_in,
    one_in,
    twist_in,
    two_in,
    col_in,
    out,
    held,
    taps,
    feeds,
    one,
    twist,
    two,
    col,
    framed,
    formed,
    sent,
    got,
    beams,
    own_sem,
    table_sem,
    halo_send,
    halo_recv,
    send_sem,
    recv_sem,
    keep_sem,
):
    me = lax.axis_index("feed")
    tm = lax.axis_index("tm")
    tm_count = lax.axis_size("tm")
    earlier = (tm + tm_count - 1) % tm_count
    later = (tm + 1) % tm_count

    own = pltpu.make_async_copy(volts, held.at[pl.ds(0, SPECTRA)], own_sem)
    own.start()
    loads = []
    for index, (src, dst) in enumerate(
        [
            (taps_in, taps),
            (feeds_in, feeds),
            (one_in, one),
            (twist_in, twist),
            (two_in, two),
            (col_in, col),
        ]
    ):
        load = pltpu.make_async_copy(src, dst, table_sem.at[index])
        load.start()
        loads.append(load)

    barrier = pltpu.get_barrier_semaphore()

    def greet(step, carry):
        pl.semaphore_signal(barrier, inc=1, device_id={"feed": (me + step) % PEERS})
        return carry

    pl.semaphore_signal(barrier, inc=1, device_id={"tm": earlier})
    pl.semaphore_signal(barrier, inc=1, device_id={"tm": later})
    lax.fori_loop(1, PEERS, greet, 0)
    pl.semaphore_wait(barrier, PEERS + 1)

    def halo(block, chunk):
        rows = pl.ds(chunk * CHUNK, CHUNK)
        return pltpu.make_async_remote_copy(
            src_ref=volts.at[block, rows],
            dst_ref=held.at[SPECTRA + block, rows],
            send_sem=halo_send.at[block, chunk],
            recv_sem=halo_recv.at[block, chunk],
            device_id={"tm": earlier},
        )

    for block in range(SPECTRA):
        for chunk in range(CHUNKS):
            halo(block, chunk).start()

    own.wait()
    for load in loads:
        load.wait()
    inside = jnp.where(tm == tm_count - 1, 0.0, 1.0).astype(F32)

    def message(spectrum, chunk, peer):
        return pltpu.make_async_remote_copy(
            src_ref=sent.at[spectrum, chunk, pl.ds(2 * peer, 2)],
            dst_ref=got.at[spectrum, :, pl.ds((chunk * PEERS + me) * ROWS, ROWS)],
            send_sem=send_sem.at[spectrum, chunk],
            recv_sem=recv_sem.at[spectrum, chunk],
            device_id={"feed": peer},
        )

    def keep(spectrum, chunk):
        return pltpu.make_async_copy(
            sent.at[spectrum, chunk, pl.ds(2 * me, 2)],
            got.at[spectrum, :, pl.ds((chunk * PEERS + me) * ROWS, ROWS)],
            keep_sem.at[spectrum, chunk],
        )

    def unit(spectrum, chunk):
        rows = pl.ds(pl.multiple_of(chunk * CHUNK, CHUNK), CHUNK)
        halo(spectrum, chunk).wait_recv()

        def filtered(step, carry):
            for inner in range(8):
                section = step * 8 + inner
                lanes = pl.ds(pl.multiple_of(section * TWO, TWO), TWO)
                total = None
                for tap in range(4):
                    weight = taps[tap : tap + 1, lanes]
                    if spectrum + tap >= SPECTRA:
                        weight = weight * inside
                    term = weight * held[spectrum + tap, rows, lanes].astype(F32)
                    total = term if total is None else total + term
                framed[pl.ds(section, CHUNK, stride=ONE), :] = total
            return carry

        lax.fori_loop(0, ONE // 8, filtered, 0)

        def formed_pair(pair, carry):
            start = pl.multiple_of(pair * 2 * ONE, 2 * ONE)
            both = framed[pl.ds(start, 2 * ONE), :].astype(BF16)
            both = jnp.concatenate([both[:ONE], both[ONE:]], axis=1)
            first = jnp.dot(one[...], both, preferred_element_type=F32)
            twist_re, twist_im = twist[0], twist[1]
            turned = []
            for which in range(2):
                cols = slice(which * TWO, (which + 1) * TWO)
                re, im = first[:ONE, cols], first[ONE:, cols]
                turned_re = (re * twist_re - im * twist_im).astype(BF16)
                turned_im = (re * twist_im + im * twist_re).astype(BF16)
                turned.append(jnp.concatenate([turned_re, turned_im], axis=1))
            turned = jnp.concatenate(turned, axis=0)
            spectra = lax.dot_general(
                two[...], turned, (((1,), (1,)), ((), ())), preferred_element_type=F32
            )
            formed[pl.ds(2 * pair, TWO, stride=CHUNK), :] = spectra[:, :ONE]
            formed[pl.ds(2 * pair + 1, TWO, stride=CHUNK), :] = spectra[:, ONE:]
            return carry

        lax.fori_loop(0, CHUNK // 2, formed_pair, 0)

        def packed(step, carry):
            for inner in range(4):
                row = step * 4 + inner
                start = pl.multiple_of(row * ROWS, ROWS)
                sent[spectrum, chunk, row] = formed[pl.ds(start, ROWS), :].astype(BF16)
            return carry

        lax.fori_loop(0, 2 * PEERS // 4, packed, 0)

        message(spectrum, chunk, peer_at(me, 1, 0)).start()

        def spread(step, carry):
            far = RING // 2 - (step + 1) // 2
            dz = jnp.where(step % 2 == 0, far, RING - far)
            message(spectrum, chunk, peer_at(me, 0, dz)).start()
            message(spectrum, chunk, peer_at(me, 1, dz)).start()
            return carry

        lax.fori_loop(0, RING - 1, spread, 0)
        keep(spectrum, chunk).start()

    def units(spectrum):
        def body(chunk, carry):
            unit(spectrum, chunk)
            return carry

        lax.fori_loop(0, CHUNKS, body, 0)

    def build(tile, carry):
        at = lax.broadcasted_iota(jnp.int32, (256, COL_FEEDS), 0) + tile * 256
        chunk, rest = at // (PEERS * ROWS), at % (PEERS * ROWS)
        feed = (rest // ROWS) * FEEDS + chunk * CHUNK + rest % CHUNK
        lane = lax.broadcasted_iota(jnp.int32, (COL_FEEDS, 256), 1)
        real = (lane // CHUNK) % 2 == 0
        upper, lower = [], []
        for r in range(CYLINDERS):
            row = jnp.concatenate([feeds[2 * r : 2 * r + 1], feeds[2 * r + 1 : 2 * r + 2]], axis=1)
            hot = jnp.where(row == feed, 1.0, 0.0).astype(BF16)
            moved = lax.dot_general(
                col[...], hot, (((1,), (1,)), ((), ())), preferred_element_type=F32
            )
            re, im = moved[:COL_FEEDS], moved[COL_FEEDS:]
            upper.append(jnp.where(real, re, -im))
            lower.append(jnp.where(real, im, re))
        cols = pl.ds(pl.multiple_of(tile * 256, 256), 256)
        for m in range(CYLINDERS):
            top = bottom = None
            for r in range(CYLINDERS):
                turn = m * r % 4
                a, c = upper[r], lower[r]
                a, c = [(a, c), (c, -a), (-a, -c), (-c, a)][turn]
                top = a if top is None else top + a
                bottom = c if bottom is None else bottom + c
            beams[0, pl.ds(m * COL_FEEDS, COL_FEEDS), cols] = top.astype(BF16)
            beams[1, pl.ds(m * COL_FEEDS, COL_FEEDS), cols] = bottom.astype(BF16)
        return carry

    def arrived(spectrum):
        for chunk in range(CHUNKS):
            rows = pl.ds(chunk * PEERS * ROWS, (PEERS - 1) * ROWS)
            part = got.at[spectrum, :, rows]
            pltpu.make_async_copy(part, part, recv_sem.at[spectrum, chunk]).wait()
            keep(spectrum, chunk).wait()

    def beam(spectrum):
        arrived(spectrum)

        def body(tile, carry):
            rows = pl.ds(pl.multiple_of(tile * 256, 256), 256)
            right = jnp.concatenate([got[spectrum, 0], got[spectrum, 1]], axis=1)
            re = jnp.dot(beams[0, rows, :], right, preferred_element_type=F32)
            im = jnp.dot(beams[1, rows, :], right, preferred_element_type=F32)
            power = re * re + im * im
            if spectrum == 0:
                out[0, rows, :] = power
            else:
                out[0, rows, :] += power
            return carry

        lax.fori_loop(0, BEAMS // 256, body, 0)

    units(0)
    lax.fori_loop(0, DEPTH // 256, build, 0)
    units(1)
    beam(0)
    units(2)
    beam(1)
    beam(2)

    for block in range(SPECTRA):
        for chunk in range(CHUNKS):
            halo(block, chunk).wait_send()
            part = sent.at[block, chunk, pl.ds(0, 2 * (PEERS - 1))]
            pltpu.make_async_copy(part, part, send_sem.at[block, chunk]).wait()


def on_device(voltages, pfb_taps, feed_of_slot):
    one, twist, two, col = constants()
    anywhere = pl.BlockSpec(memory_space=pl.ANY)
    dma = pltpu.SemaphoreType.DMA
    return pl.pallas_call(
        kernel,
        out_shape=jax.ShapeDtypeStruct((1, BEAMS, 2 * ONE), F32),
        in_specs=[anywhere] * 7,
        out_specs=pl.BlockSpec(memory_space=pltpu.VMEM),
        scratch_shapes=[
            pltpu.VMEM((2 * SPECTRA, FEEDS, BLOCK), BF16),
            pltpu.VMEM((4, BLOCK), F32),
            pltpu.VMEM((8, 128), jnp.int32),
            pltpu.VMEM((2 * ONE, ONE), BF16),
            pltpu.VMEM((2, ONE, TWO), F32),
            pltpu.VMEM((TWO, 2 * TWO), BF16),
            pltpu.VMEM((2 * COL_FEEDS, COL_FEEDS), BF16),
            pltpu.VMEM((CHUNK * ONE, TWO), F32),
            pltpu.VMEM((TWO * CHUNK, ONE), F32),
            pltpu.VMEM((SPECTRA, CHUNKS, 2 * PEERS, ROWS, ONE), BF16),
            pltpu.VMEM((SPECTRA, 2, DEPTH, ONE), BF16),
            pltpu.VMEM((2, BEAMS, DEPTH), BF16),
            dma,
            dma((6,)),
            dma((SPECTRA, CHUNKS)),
            dma((SPECTRA, CHUNKS)),
            dma((SPECTRA, CHUNKS)),
            dma((SPECTRA, CHUNKS)),
            dma((SPECTRA, CHUNKS)),
        ],
        compiler_params=pltpu.CompilerParams(
            collective_id=0, has_side_effects=True, vmem_limit_bytes=52 * 1024 * 1024
        ),
        name="channel_beams",
    )(voltages, pfb_taps, feed_of_slot.reshape(8, 128), one, twist, two, col)


def solution(mesh):
    in_specs = (P("tm", "feed", None), P(), P())
    out_specs = P("tm", None, "feed")
    return jax.shard_map(
        on_device, mesh=mesh, in_specs=in_specs, out_specs=out_specs, check_vma=False
    )
```

time: 287 us -> 170 us (0.59)
  the two profiles are of different devices: /device:TPU:49 before, /device:TPU:1 now
where the time goes in v1:
time: 170 us
  Pallas kernels  164 us (96%)
  local copies, waits for them, and re-layouts  6.14 us (4%)
    pallas_call x1, Pallas kernels, on_device(): pl.pallas_call(kernel, out_shape=jax.ShapeDtypeStruct((1, BEAMS, 2 * ONE)...  164 us
    unnamed x13, local copies, waits for them, and re-layouts  6.14 us

profile of v1, /device:TPU:1, one launch (start us, length us, event | category | flops | bytes accessed | tf_op | source)
XLA Modules:
  0.0 169.8 jit_solution(9216699058303424019)
XLA Ops:
  0.0 0.0 copy-start
  0.0 0.9 copy-done
  1.0 0.0 copy-start.1
  1.0 0.9 copy-done.1
  1.9 0.0 copy-start.2
  1.9 0.9 copy-done.2
  2.8 0.0 copy-start.3
  2.8 0.8 copy-done.3
  3.6 0.0 copy-start.4
  3.6 0.8 copy-done.4
  4.5 0.0 copy-start.5
  4.5 0.7 copy-done.5
  5.2 163.7 %channel_beams.1 = f32[1,1024,256]{2,1,0:T(8,128)S(1)} custom-call(bf16[3,32,16384]{2,1,0:T(8,128)(2,1)} %volts.1, f32[4,16384]{1,0:T(4,128)S(1)} %copy-done, s32[8,128]{1,0:T(8,128)S(1)} %bitcast.1, bf16[256,128]{1,0:T(8,128)(2,1)S(1)} %copy-done.4, f32[2,128,128]{2,1,0:T(8,128)S(1)} %copy-done.2, bf16[128,256]{1,0:T(8,128)(2,1)S(1)} %copy-done.3, ...), custom_call_target="tpu_custom_call" | custom-call | tf_op jit(solution)/shard_map/channel_beams/pallas_call | solution.py:301
  168.8 1.0 copy.9
Async XLA Ops:
  0.0 0.9 copy-start
  1.0 0.9 copy-start.1
  1.9 0.9 copy-start.2
  2.8 0.8 copy-start.3
  3.6 0.8 copy-start.4
  4.5 0.7 copy-start.5
